TPU v7x, 32 devices: a whole 2x2x4 slice. The times are simulated.
32 devices in a mesh: groups: 2 (over y), word: 4 (over z), sub: 4 (over x, core).
Axes of the slice: x: 2, y: 2, z: 4, core: 2. Of those that a mesh axis runs over, the one named last changes fastest.
Arguments:
- word_ids: int32 [4, 32, 512], P('word', None, 'groups'), parts along dimension 2, may hold values from 0 to 32767
- word_weights: float32 [4, 32, 512], P('word', None, 'groups'), parts along dimension 2, may hold values from 0.25 to 12
- neighbours: int32 [50, 512], P(None, 'groups'), parts along dimension 1, may hold values from 0 to 255
- descriptors: bfloat16 [512, 128, 128], P(('groups', 'word'), 'sub'), parts along dimension 0, may hold values from -6 to 6
- keypoint_count: int32 [512], P('groups'), parts along dimension 0, may hold values from 32 to 128
- send_table: int32 [8, 4, 4, 2], P('groups'), parts along dimension 0, may hold values from 0 to 63
- pair_slots: int32 [8, 4, 32, 2], P(('groups', 'word'), 'sub'), parts along dimension 0, may hold values from 0 to 7, as said below
Outputs:
- similarity: float32 [512, 50], P(('groups', 'word', 'sub')), parts along dimension 0
- nearest: float32 [8, 4, 32, 128], P(('groups', 'word'), 'sub'), parts along dimension 0
- margin: float32 [8, 4, 32, 128], P(('groups', 'word'), 'sub'), parts along dimension 0
There are 2 independent parts, one for each index of `groups`. A program takes and returns all parts, laid end to end along the dimension named above; each array names one. Nothing has to cross between parts.
Inputs may be any that keep to these rules, and one draw needn't show every extreme that they name: `word_ids`: each image has 32 word occurrences in every vocabulary shard, given as word numbers within that shard; a number may repeat. `keypoint_count`: keypoint slots at and beyond an image's count are padding. send_table[v, w, s, c] is an image counted among word index v's 64 stored images; every device receives exactly 2 images from every word index, and one image may go to many devices. `pair_slots`: the two slots of a pair are different slots among the 8 of that device, the query first.
All inputs are finite; a program needn't handle non-finite values.
Results may differ from a plain program's by a relative error of at most 0.0003.
Values may be sent and summed in bfloat16 or wider, within the bound.
A program may use at most 64 MiB of HBM per device.

v0:
```python
import functools

import jax
import jax.numpy as jnp
from jax import lax
from jax.experimental import pallas as pl
from jax.experimental.pallas import tpu as pltpu
from jax.sharding import PartitionSpec as P

MESH = pl.DeviceIdType.MESH
LANES = 128
LIMIT = 40 * 1024 * 1024
F32, BF16, I32 = jnp.float32, jnp.bfloat16, jnp.int32


def ceil_to(value, step):
    return (value + step - 1) // step * step


def loop(count, limit, body):
    if count <= limit:
        for i in range(count):
            body(i)
    else:
        lax.fori_loop(0, count, lambda i, carry: (body(i), carry)[1], 0)


def pieces(x):
    first = x.astype(BF16)
    rest = x - first.astype(F32)
    second = rest.astype(BF16)
    third = (rest - second.astype(F32)).astype(BF16)
    return first, second, third


def dot(a, b):
    return lax.dot_general(a, b, (((1,), (0,)), ((), ())), preferred_element_type=F32)


def onehot(want, rows):
    numbers = lax.broadcasted_iota(I32, (rows, want.shape[-1]), 0)
    return jnp.where(numbers == want, F32(1.0), F32(0.0)).astype(BF16)


def kernel(
    W, S, dims,
    ids_hbm, wts_hbm, nb_hbm, desc_hbm, cnt_hbm, tab_hbm, slot_hbm,
    sim_ref, near_ref, marg_ref,
    ids_ref, wts_ref, nb_ref, desc_ref, cnt_ref, to_ref, from_ref, slot_ref,
    outd, held, table, nbf, own, hot, got, part_out, part_in,
    qs, rt, sqb, info, low_s, next_s, info_s,
    dsend, drecv, psend, precv, inputs,
):
    B, I, K, R, KK, J, C, TR, KP, NP, H = dims
    me_g, me_w, me_s = lax.axis_index("groups"), lax.axis_index("word"), lax.axis_index("sub")
    n = W * S
    stored, feats, width = desc_ref.shape

    def turn(step):
        if W & (W - 1):
            return (me_w + step) % W
        word, bit = me_w, 1
        while bit < W:
            word += step // bit % 2 * (1 - me_w // bit % 2 * 2) * bit
            bit *= 2
        return word

    def peer(q):
        return turn(q // S), (me_s + q % S) % S

    barrier = pltpu.get_barrier_semaphore()

    def greet(i):
        w, s = peer(i + 1)
        pl.semaphore_signal(barrier, inc=1, device_id=(me_g, w, s), device_id_type=MESH)

    loop(n - 1, 16, greet)

    loads = [
        pltpu.make_async_copy(source, target, inputs.at[i])
        for i, (source, target) in enumerate((
            (tab_hbm.at[me_w], to_ref),
            (desc_hbm, desc_ref),
            (ids_hbm, ids_ref),
            (wts_hbm, wts_ref),
            (nb_hbm, nb_ref),
            (tab_hbm.at[:, me_w], from_ref),
            (cnt_hbm, cnt_ref),
            (slot_hbm, slot_ref),
        ))
    ]
    for load in loads:
        load.start()
    for load in loads:
        load.wait()

    def pick(q):
        w, s = peer(q)
        for c in range(C):
            outd[q, c] = desc_ref[to_ref[w, c, s]]

    loop(n, 16, pick)
    for c in range(C):
        held[me_w, me_s, c] = desc_ref[to_ref[me_w, c, me_s]]

    ids = ids_ref[...]
    table[0:B] = (ids >> 8).astype(F32).astype(BF16)
    table[B : 2 * B] = (ids & 255).astype(F32).astype(BF16)
    for i, piece in enumerate(pieces(wts_ref[...])):
        table[(2 + i) * B : (3 + i) * B] = piece
    nbf[...] = jnp.zeros_like(nbf)
    nbf[0:K] = nb_ref[...]
    near_ids = nbf[...]
    table[TR : TR + KP] = (near_ids >> 8).astype(F32).astype(BF16)
    table[TR + KP : TR + 2 * KP] = (near_ids & 255).astype(F32).astype(BF16)

    chunk = min(I, 256)

    def self_norm(i):
        at = pl.ds(i * chunk if isinstance(i, int) else pl.multiple_of(i * chunk, chunk), chunk)
        here = ids_ref[:, at]
        total = jnp.zeros((B, chunk), F32)
        for a in range(B):
            total += jnp.where(here == ids_ref[a : a + 1, at], wts_ref[a : a + 1, at], F32(0.0))
        norm = jnp.sum(total * wts_ref[:, at], axis=0, keepdims=True)
        row = lax.broadcasted_iota(I32, (16, chunk), 0)
        block = jnp.zeros((16, chunk), F32)
        for k, piece in enumerate(pieces(norm)):
            block = jnp.where(row == k, piece.astype(F32), block)
        table[5 * B : TR, at] = block.astype(BF16)

    loop(I // chunk, 1, self_norm)

    pl.semaphore_wait(barrier, n - 1)

    def desc_copy(q):
        w, s = peer(q)
        return pltpu.make_async_remote_copy(
            src_ref=outd.at[q], dst_ref=held.at[me_w, me_s],
            send_sem=dsend.at[q], recv_sem=drecv.at[me_w * S + me_s],
            device_id=(me_g, w, s), device_id_type=MESH,
        )

    loop(n - 1, 16, lambda i: desc_copy(1 + (i + (W // 2 * S - 1)) % (n - 1)).start())

    def part_copy(d):
        return pltpu.make_async_remote_copy(
            src_ref=part_out.at[d], dst_ref=part_in.at[d],
            send_sem=psend.at[d], recv_sem=precv.at[d],
            device_id=(me_g, (me_w + 1 + d) % W, me_s), device_id_type=MESH,
        )

    lane = lax.broadcasted_iota(I32, (1, LANES), 1)
    digit = lax.broadcasted_iota(I32, (KK, LANES), 0) == lax.broadcasted_iota(I32, (KK, LANES), 1) // R

    def target(d):
        w = (me_w + 1 + d) % W
        mine = dot(table[...], onehot((w * S + me_s) * R + lane % R, I))
        own[0:B] = mine[0:B] * 256.0 + mine[B : 2 * B]
        own[B : 2 * B] = mine[2 * B : 3 * B] + mine[3 * B : 4 * B] + mine[4 * B : 5 * B]
        listed = mine[TR : TR + KP] * 256.0 + mine[TR + KP : TR + 2 * KP]
        for j in range(J):
            chosen = jnp.where(digit, listed[j * KK : (j + 1) * KK], F32(0.0))
            want = jnp.sum(chosen, axis=0, keepdims=True).astype(I32)
            hot[:, j * LANES : (j + 1) * LANES] = onehot(want, I)
        got[...] = dot(table[0:TR], hot[...])
        cols = [slice(j * LANES, (j + 1) * LANES) for j in range(J)]
        other = [got[0:B, c] * 256.0 + got[B : 2 * B, c] for c in cols]
        total = [jnp.zeros((B, LANES), F32) for c in cols]
        for a in range(B):
            word, weight = own[a : a + 1], own[B + a : B + a + 1]
            for j in range(J):
                total[j] += jnp.where(other[j] == word, weight, F32(0.0))
        for j, c in enumerate(cols):
            values = got[2 * B : 3 * B, c] + got[3 * B : 4 * B, c] + got[4 * B : 5 * B, c]
            part_out[d, j : j + 1] = jnp.sum(total[j] * values, axis=0, keepdims=True)
            norms = got[5 * B : 5 * B + 1, c] + got[5 * B + 1 : 5 * B + 2, c] + got[5 * B + 2 : 5 * B + 3, c]
            part_out[d, J + j : J + j + 1] = norms
        part_out[d, 2 * J : 2 * J + 1] = (
            mine[5 * B : 5 * B + 1] + mine[5 * B + 1 : 5 * B + 2] + mine[5 * B + 2 : 5 * B + 3]
        )
        if isinstance(d, int):
            if d >= 1:
                part_copy(d - 1).start()
        else:
            @pl.when(d >= 1)
            def _():
                part_copy(d - 1).start()

    loop(W, 4, target)

    def arrive(i):
        w = turn(i)

        def slice_wait(j):
            s = (me_s + j) % S
            pltpu.make_async_remote_copy(
                src_ref=outd.at[0], dst_ref=held.at[w, s],
                send_sem=dsend.at[0], recv_sem=drecv.at[w * S + s],
                device_id=(me_g, w, s), device_id_type=MESH,
            ).wait_recv()

        for j in range(S):
            if isinstance(i, int):
                if i > 0 or j > 0:
                    slice_wait(j)
            elif j > 0:
                slice_wait(j)
            else:
                @pl.when(i > 0)
                def _():
                    slice_wait(0)
        for c in range(C):
            h = w * C + c
            full = jnp.concatenate([held[w, s, c] for s in range(S)], axis=0)
            qs[h] = full
            wide = full.astype(F32)
            turned = jnp.transpose(wide)
            rt[h] = (turned * -2.0).astype(BF16)
            count = cnt_ref[w * stored + from_ref[w, c, me_s]]
            down = lax.broadcasted_iota(I32, (width, width), 0)
            square = jnp.sum(turned * turned, axis=1, keepdims=True)
            sqb[h] = jnp.where(down < count, square, F32(1e30))
            flat = jnp.sum(wide * wide, axis=0, keepdims=True)
            live = jnp.where(lax.broadcasted_iota(I32, (8, width), 1) < count, F32(1.0), F32(0.0))
            info[h] = jnp.where(lax.broadcasted_iota(I32, (8, width), 0) == 0, flat, live)

    loop(W, 4, arrive)

    pairs = near_ref.shape[0]
    group = 8

    def match(i):
        for k in range(group):
            p = i * group + k
            q, r = slot_ref[0, p], slot_ref[1, p]
            inner = dot(rt[r], qs[q])
            base = sqb[r]
            tops = []
            for t in range(2):
                low = second = None
                for v in range(t, width // 8, 2):
                    x = base[v * 8 : v * 8 + 8] + inner[v * 8 : v * 8 + 8]
                    if low is None:
                        low = x
                    elif second is None:
                        low, second = jnp.minimum(low, x), jnp.maximum(low, x)
                    else:
                        second = jnp.minimum(second, jnp.maximum(low, x))
                        low = jnp.minimum(low, x)
                tops.append((low, second))
            (l0, s0), (l1, s1) = tops
            at = pl.ds(p * 8, 8)
            low_s[at] = jnp.minimum(l0, l1)
            next_s[at] = jnp.minimum(jnp.maximum(l0, l1), jnp.minimum(s0, s1))
            info_s[at] = info[q]

    loop(pairs // group, 4, match)

    rows = [pl.ds(i, pairs, stride=8) for i in range(8)]
    low, second = low_s[rows[0]], next_s[rows[0]]
    for at in rows[1:]:
        l1, s1 = low_s[at], next_s[at]
        second = jnp.minimum(jnp.maximum(low, l1), jnp.minimum(second, s1))
        low = jnp.minimum(low, l1)
    live = info_s[rows[1]] > 0.0
    features = F32(feats * S)
    near_ref[...] = jnp.where(live, (low + info_s[rows[0]]) / features, F32(0.0))
    marg_ref[...] = jnp.where(live, (second - low) / features, F32(0.0))

    loop(W - 1, 4, lambda d: part_copy(d).wait_recv())
    total = part_out[W - 1]
    for d in range(W - 1):
        total += part_in[d]
    cosine = total[0:J] / jnp.sqrt(total[2 * J : 2 * J + 1] * total[J : 2 * J])
    spread = lax.broadcasted_iota(I32, (R, LANES), 1) % R == lax.broadcasted_iota(I32, (R, LANES), 0)
    out_cols = ceil_to(K, LANES)
    deep = lax.broadcasted_iota(I32, (LANES, out_cols), 0) // R
    across = lax.broadcasted_iota(I32, (LANES, out_cols), 1)
    result = jnp.zeros((R, out_cols), F32)
    for j in range(J):
        place = jnp.where(across == deep + j * KK, F32(1.0), F32(0.0)).astype(BF16)
        for piece in pieces(jnp.where(spread, cosine[j : j + 1], F32(0.0))):
            result += dot(piece, place)
    sim_ref[...] = result[:, 0:K]

    loop(n - 1, 16, lambda i: desc_copy(i + 1).wait_send())
    loop(W - 1, 4, lambda d: part_copy(d).wait_send())


def finish(*refs):
    sems = refs[6]
    copies = [pltpu.make_async_copy(refs[i], refs[3 + i], sems.at[i]) for i in range(3)]
    for copy in copies:
        copy.start()
    for copy in copies:
        copy.wait()


def local(W, S, word_ids, word_weights, neighbours, descriptors, keypoint_count, send_table, pair_slots):
    B, I = word_ids.shape[1:]
    K = neighbours.shape[0]
    R = I // (W * S)
    KK = LANES // R
    J = -(-K // KK)
    C = send_table.shape[-1]
    TR = ceil_to(5 * B + 3, 16)
    KP = ceil_to(J * KK, 16)
    NP = ceil_to(2 * J + 1, 8)
    H = W * C
    stored, feats, width = descriptors.shape
    pairs = pair_slots.shape[2]
    vmem = pl.BlockSpec(memory_space=pltpu.VMEM)
    results = ((R, K), (pairs, width), (pairs, width))
    parts = pl.pallas_call(
        functools.partial(kernel, W, S, (B, I, K, R, KK, J, C, TR, KP, NP, H)),
        out_shape=tuple(pltpu.VMEM(shape, F32) for shape in results),
        in_specs=[pl.BlockSpec(memory_space=pltpu.HBM)] * 7,
        out_specs=(vmem, vmem, vmem),
        scratch_shapes=[
            pltpu.VMEM((B, I), I32),
            pltpu.VMEM((B, I), F32),
            pltpu.VMEM((K, I), I32),
            pltpu.VMEM(descriptors.shape, BF16),
            pltpu.SMEM(keypoint_count.shape, I32),
            pltpu.SMEM((W, C, S), I32),
            pltpu.SMEM((W, C, S), I32),
            pltpu.SMEM((2, pairs), I32),
            pltpu.VMEM((W * S, C, feats, width), BF16),
            pltpu.VMEM((W, S, C, feats, width), BF16),
            pltpu.VMEM((TR + 2 * KP, I), BF16),
            pltpu.VMEM((KP, I), I32),
            pltpu.VMEM((2 * B, LANES), F32),
            pltpu.VMEM((I, J * LANES), BF16),
            pltpu.VMEM((TR, J * LANES), F32),
            pltpu.VMEM((W, NP, LANES), F32),
            pltpu.VMEM((W, NP, LANES), F32),
            pltpu.VMEM((H, width, width), BF16),
            pltpu.VMEM((H, width, width), BF16),
            pltpu.VMEM((H, width, width), F32),
            pltpu.VMEM((H, 8, width), F32),
            pltpu.VMEM((pairs * 8, width), F32),
            pltpu.VMEM((pairs * 8, width), F32),
            pltpu.VMEM((pairs * 8, width), F32),
            pltpu.SemaphoreType.DMA((W * S,)),
            pltpu.SemaphoreType.DMA((W * S,)),
            pltpu.SemaphoreType.DMA((W,)),
            pltpu.SemaphoreType.DMA((W,)),
            pltpu.SemaphoreType.DMA((8,)),
        ],
        compiler_params=pltpu.CompilerParams(
            collective_id=0, has_side_effects=True, vmem_limit_bytes=LIMIT
        ),
    )(*(pltpu.with_memory_space_constraint(operand, pltpu.HBM) for operand in (
        word_ids[0], word_weights[0], neighbours, descriptors,
        keypoint_count, jnp.swapaxes(send_table, 2, 3), jnp.swapaxes(pair_slots, 2, 3)[0, 0],
    )))
    similarity, nearest, margin = pl.pallas_call(
        finish,
        out_shape=tuple(jax.ShapeDtypeStruct(shape, F32) for shape in results),
        in_specs=[pl.BlockSpec(memory_space=pl.ANY)] * 3,
        out_specs=(pl.BlockSpec(memory_space=pltpu.HBM),) * 3,
        scratch_shapes=[pltpu.SemaphoreType.DMA((3,))],
        compiler_params=pltpu.CompilerParams(vmem_limit_bytes=LIMIT),
    )(*parts)
    return similarity, nearest[None, None], margin[None, None]


def solution(mesh):
    in_specs = (
        P("word", None, "groups"),
        P("word", None, "groups"),
        P(None, "groups"),
        P(("groups", "word"), "sub", None),
        P("groups"),
        P("groups", None, None, None),
        P(("groups", "word"), "sub", None, None),
    )
    out_specs = (
        P(("groups", "word", "sub"), None),
        P(("groups", "word"), "sub", None, None),
        P(("groups", "word"), "sub", None, None),
    )
    body = functools.partial(local, mesh.shape["word"], mesh.shape["sub"])
    return jax.shard_map(body, mesh=mesh, in_specs=in_specs, out_specs=out_specs, check_vma=False)
```

profile of v0, /device:TPU:0, one launch (start us, length us, event | category | flops | bytes accessed | tf_op | source)
XLA Modules:
  0.0 16.0 jit_solution(3404065860500989092)
XLA Ops:
  0.6 14.7 %shard_map.94 = (f32[16,50]{1,0:T(8,128)S(1)}, f32[32,128]{1,0:T(8,128)S(1)}, f32[32,128]{1,0:T(8,128)S(1)}) custom-call(s32[32,256]{1,0:T(8,128)} %bitcast.8, f32[32,256]{1,0:T(8,128)} %bitcast.9, s32[50,256]{1,0:T(8,128)} %nb_hbm.1, bf16[64,32,128]{2,1,0:T(8,128)(2,1)} %desc_hbm.1, s32[256]{0:T(256)} %cnt_hbm.1, s32[4,4,2,4]{3,2,1,0:T(2,128)} %bitcast.10, ...), custom_call_target="tpu_custom_call" | custom-call | tf_op jit(solution)/shard_map/pallas_call | solution.py:315
  15.4 0.6 %shard_map.95 = (f32[16,50]{1,0:T(8,128)}, f32[32,128]{1,0:T(8,128)}, f32[32,128]{1,0:T(8,128)}) custom-call(f32[16,50]{1,0:T(8,128)S(1)} %get-tuple-element.9.refs_0_, f32[32,128]{1,0:T(8,128)S(1)} %get-tuple-element.10.refs_1_, f32[32,128]{1,0:T(8,128)S(1)} %get-tuple-element.11.refs_2_), custom_call_target="tpu_custom_call" | custom-call | tf_op jit(solution)/shard_map/pallas_call | solution.py:358
where the time goes:
time: 16.2 us; the launch traced here: 16 us
  Pallas kernels  15.4 us (95%)
  between operations  0.64 us (4%)
    pallas_call x1, Pallas kernels, local(): pl.pallas_call(functools.partial(kernel, W, S, (B, I, K, R, KK, J, C, TR,...  14.7 us
    pallas_call x1, Pallas kernels, local(): pl.pallas_call(finish, out_shape=tuple((jax.ShapeDtypeStruct(shape, F32)...  0.64 us

commit v1 on v0

--- a/solution.py
+++ b/solution.py
@@ -49,7 +49,7 @@
     ids_ref, wts_ref, nb_ref, desc_ref, cnt_ref, to_ref, from_ref, slot_ref,
     outd, held, table, nbf, own, hot, got, part_out, part_in,
     qs, rt, sqb, info, low_s, next_s, info_s,
-    dsend, drecv, psend, precv, inputs,
+    dsend, drecv, psend, precv, inputs, go,
 ):
     B, I, K, R, KK, J, C, TR, KP, NP, H = dims
     me_g, me_w, me_s = lax.axis_index("groups"), lax.axis_index("word"), lax.axis_index("sub")
@@ -65,43 +65,80 @@
             bit *= 2
         return word
 
-    def peer(q):
-        return turn(q // S), (me_s + q % S) % S
+    def word_at(k):
+        return k + jnp.where(me_w <= k, 1, 0)
+
+    def near(j):
+        return (me_s + 1 + j) % S
+
+    def load(sem, source, target):
+        return pltpu.make_async_copy(source, target, inputs.at[sem])
+
+    first = [
+        load(0, tab_hbm.at[me_w], to_ref),
+        load(1, desc_hbm, desc_ref),
+    ]
+    rest = [
+        load(2, ids_hbm, ids_ref),
+        load(3, wts_hbm, wts_ref),
+        load(4, nb_hbm, nb_ref),
+        load(5, tab_hbm.at[:, me_w], from_ref),
+        load(6, cnt_hbm, cnt_ref),
+        load(7, slot_hbm, slot_ref),
+    ]
+    for copy in first:
+        copy.start()
+
+    def words(above, body):
+        for_each = lambda k: pl.when((k >= me_w) if above else (k < me_w))(lambda: body(word_at(k)))
+        loop(W - 1, 4, for_each)
+
+    def subs(above, body):
+        loop(S, 8, lambda s: pl.when((s > me_s) if above else (s < me_s))(lambda: body(s)))
 
     barrier = pltpu.get_barrier_semaphore()
 
-    def greet(i):
-        w, s = peer(i + 1)
-        pl.semaphore_signal(barrier, inc=1, device_id=(me_g, w, s), device_id_type=MESH)
-
-    loop(n - 1, 16, greet)
-
-    loads = [
-        pltpu.make_async_copy(source, target, inputs.at[i])
-        for i, (source, target) in enumerate((
-            (tab_hbm.at[me_w], to_ref),
-            (desc_hbm, desc_ref),
-            (ids_hbm, ids_ref),
-            (wts_hbm, wts_ref),
-            (nb_hbm, nb_ref),
-            (tab_hbm.at[:, me_w], from_ref),
-            (cnt_hbm, cnt_ref),
-            (slot_hbm, slot_ref),
-        ))
-    ]
-    for load in loads:
-        load.start()
-    for load in loads:
-        load.wait()
-
-    def pick(q):
-        w, s = peer(q)
+    def signal(sem, w, s):
+        pl.semaphore_signal(sem, inc=1, device_id=(me_g, w, s), device_id_type=MESH)
+
+    subs(True, lambda s: signal(barrier, me_w, s))
+    words(True, lambda w: loop(S, 8, lambda s: signal(barrier, w, s)))
+    for copy in rest:
+        copy.start()
+    lower = me_w * S + me_s
+    pl.when(lower > 0)(lambda: pl.semaphore_wait(barrier, lower))
+    words(False, lambda w: loop(S, 8, lambda s: signal(go.at[me_w], w, s)))
+    subs(False, lambda s: signal(go.at[me_w], me_w, s))
+    for copy in first:
+        copy.wait()
+
+    def pick(slot, w, s):
         for c in range(C):
-            outd[q, c] = desc_ref[to_ref[w, c, s]]
-
-    loop(n, 16, pick)
+            outd[slot, c] = desc_ref[to_ref[w, c, s]]
+
+    loop(W - 1, 4, lambda k: loop(S, 8, lambda s: pick(k * S + s, word_at(k), s)))
+    loop(S, 8, lambda s: pick((W - 1) * S + s, me_w, s))
     for c in range(C):
         held[me_w, me_s, c] = desc_ref[to_ref[me_w, c, me_s]]
+
+    def send(slot, w, s):
+        pltpu.make_async_remote_copy(
+            src_ref=outd.at[slot], dst_ref=held.at[me_w, me_s],
+            send_sem=dsend, recv_sem=drecv.at[me_w],
+            device_id=(me_g, w, s), device_id_type=MESH,
+        ).start()
+
+    def send_word(k):
+        loop(S, 8, lambda s: send(k * S + s, word_at(k), s))
+
+    def send_near(s):
+        send((W - 1) * S + s, me_w, s)
+
+    pl.when(me_w > 0)(lambda: send_word(0))
+    subs(False, send_near)
+
+    for copy in rest:
+        copy.wait()
 
     ids = ids_ref[...]
     table[0:B] = (ids >> 8).astype(F32).astype(BF16)
@@ -131,30 +168,26 @@
 
     loop(I // chunk, 1, self_norm)
 
-    pl.semaphore_wait(barrier, n - 1)
-
-    def desc_copy(q):
-        w, s = peer(q)
+    def part_copy(d):
+        w = word_at(d)
         return pltpu.make_async_remote_copy(
-            src_ref=outd.at[q], dst_ref=held.at[me_w, me_s],
-            send_sem=dsend.at[q], recv_sem=drecv.at[me_w * S + me_s],
-            device_id=(me_g, w, s), device_id_type=MESH,
+            src_ref=part_out.at[d], dst_ref=part_in.at[me_w - jnp.where(me_w > w, 1, 0)],
+            send_sem=psend, recv_sem=precv,
+            device_id=(me_g, w, me_s), device_id_type=MESH,
         )
 
-    loop(n - 1, 16, lambda i: desc_copy(1 + (i + (W // 2 * S - 1)) % (n - 1)).start())
-
-    def part_copy(d):
-        return pltpu.make_async_remote_copy(
-            src_ref=part_out.at[d], dst_ref=part_in.at[d],
-            send_sem=psend.at[d], recv_sem=precv.at[d],
-            device_id=(me_g, (me_w + 1 + d) % W, me_s), device_id_type=MESH,
-        )
+    early = 2 * me_w < W - 1
+
+    def due(d):
+        low = jnp.logical_and(d >= 0, d < me_w)
+        high = jnp.logical_and(d >= me_w, d < W - 1)
+        return jnp.logical_or(low, jnp.logical_and(high, jnp.logical_not(early)))
 
     lane = lax.broadcasted_iota(I32, (1, LANES), 1)
     digit = lax.broadcasted_iota(I32, (KK, LANES), 0) == lax.broadcasted_iota(I32, (KK, LANES), 1) // R
 
     def target(d):
-        w = (me_w + 1 + d) % W
+        w = jnp.where(d == W - 1, me_w, word_at(d))
         mine = dot(table[...], onehot((w * S + me_s) * R + lane % R, I))
         own[0:B] = mine[0:B] * 256.0 + mine[B : 2 * B]
         own[B : 2 * B] = mine[2 * B : 3 * B] + mine[3 * B : 4 * B] + mine[4 * B : 5 * B]
@@ -163,14 +196,16 @@
             chosen = jnp.where(digit, listed[j * KK : (j + 1) * KK], F32(0.0))
             want = jnp.sum(chosen, axis=0, keepdims=True).astype(I32)
             hot[:, j * LANES : (j + 1) * LANES] = onehot(want, I)
+        pl.when(due(d - 1))(lambda: part_copy(d - 1).start())
+        pl.when(jnp.logical_and(d >= 1, d < me_w))(lambda: send_word(d))
         got[...] = dot(table[0:TR], hot[...])
         cols = [slice(j * LANES, (j + 1) * LANES) for j in range(J)]
-        other = [got[0:B, c] * 256.0 + got[B : 2 * B, c] for c in cols]
+        words_of = [got[0:B, c] * 256.0 + got[B : 2 * B, c] for c in cols]
         total = [jnp.zeros((B, LANES), F32) for c in cols]
         for a in range(B):
             word, weight = own[a : a + 1], own[B + a : B + a + 1]
             for j in range(J):
-                total[j] += jnp.where(other[j] == word, weight, F32(0.0))
+                total[j] += jnp.where(words_of[j] == word, weight, F32(0.0))
         for j, c in enumerate(cols):
             values = got[2 * B : 3 * B, c] + got[3 * B : 4 * B, c] + got[4 * B : 5 * B, c]
             part_out[d, j : j + 1] = jnp.sum(total[j] * values, axis=0, keepdims=True)
@@ -179,37 +214,50 @@
         part_out[d, 2 * J : 2 * J + 1] = (
             mine[5 * B : 5 * B + 1] + mine[5 * B + 1 : 5 * B + 2] + mine[5 * B + 2 : 5 * B + 3]
         )
-        if isinstance(d, int):
-            if d >= 1:
-                part_copy(d - 1).start()
+    def targets(first, last):
+        lax.fori_loop(first, last, lambda d, carry: (target(d), carry)[1], 0)
+
+    def quota(e):
+        return jnp.minimum(jnp.maximum(W - 2 - me_w + e, 1), W)
+
+    def stage(e):
+        targets(0 if isinstance(e, int) and e == 0 else jnp.where(e == 0, 0, quota(e - 1)), quota(e))
+        if not isinstance(e, int):
+            pl.when(e == 0)(near_stage)
+            pl.when(e > 0)(lambda: far_stage(e))
+        elif e == 0:
+            near_stage()
         else:
-            @pl.when(d >= 1)
-            def _():
-                part_copy(d - 1).start()
-
-    loop(W, 4, target)
+            far_stage(e)
+
+    def near_stage():
+        pl.when(me_s < S - 1)(lambda: pl.semaphore_wait(go.at[me_w], S - 1 - me_s))
+        subs(True, send_near)
+
+    def far_stage(e):
+        w = me_w + e
+        pl.semaphore_wait(go.at[w], S)
+        pl.when(early)(lambda: part_copy(w - 1).start())
+        send_word(w - 1)
+
+    loop(W, 4, lambda e: pl.when(me_w + e < W)(lambda: stage(e)))
+    targets(quota(W - 1 - me_w), W)
 
     def arrive(i):
         w = turn(i)
 
-        def slice_wait(j):
-            s = (me_s + j) % S
+        def arrived(slices):
             pltpu.make_async_remote_copy(
-                src_ref=outd.at[0], dst_ref=held.at[w, s],
-                send_sem=dsend.at[0], recv_sem=drecv.at[w * S + s],
-                device_id=(me_g, w, s), device_id_type=MESH,
+                src_ref=held.at[w, pl.ds(0, slices)], dst_ref=held.at[w, pl.ds(0, slices)],
+                send_sem=dsend, recv_sem=drecv.at[w],
+                device_id=(me_g, me_w, me_s), device_id_type=MESH,
             ).wait_recv()
 
-        for j in range(S):
-            if isinstance(i, int):
-                if i > 0 or j > 0:
-                    slice_wait(j)
-            elif j > 0:
-                slice_wait(j)
-            else:
-                @pl.when(i > 0)
-                def _():
-                    slice_wait(0)
+        if isinstance(i, int):
+            arrived(S if i > 0 else S - 1)
+        else:
+            pl.when(i > 0)(lambda: arrived(S))
+            pl.when(i == 0)(lambda: arrived(S - 1))
         for c in range(C):
             h = w * C + c
             full = jnp.concatenate([held[w, s, c] for s in range(S)], axis=0)
@@ -225,7 +273,31 @@
             live = jnp.where(lax.broadcasted_iota(I32, (8, width), 1) < count, F32(1.0), F32(0.0))
             info[h] = jnp.where(lax.broadcasted_iota(I32, (8, width), 0) == 0, flat, live)
 
-    loop(W, 4, arrive)
+    loop(W - 1, 4, arrive)
+
+    def whole(ref, send_sem, recv_sem):
+        return pltpu.make_async_remote_copy(
+            src_ref=ref, dst_ref=ref, send_sem=send_sem, recv_sem=recv_sem,
+            device_id=(me_g, me_w, me_s), device_id_type=MESH,
+        )
+
+    whole(part_in.at[pl.ds(0, W - 1)], psend, precv).wait_recv()
+    total = part_out[W - 1]
+    for d in range(W - 1):
+        total += part_in[d]
+    cosine = total[0:J] / jnp.sqrt(total[2 * J : 2 * J + 1] * total[J : 2 * J])
+    spread = lax.broadcasted_iota(I32, (R, LANES), 1) % R == lax.broadcasted_iota(I32, (R, LANES), 0)
+    out_cols = ceil_to(K, LANES)
+    deep = lax.broadcasted_iota(I32, (LANES, out_cols), 0) // R
+    across = lax.broadcasted_iota(I32, (LANES, out_cols), 1)
+    result = jnp.zeros((R, out_cols), F32)
+    for j in range(J):
+        place = jnp.where(across == deep + j * KK, F32(1.0), F32(0.0)).astype(BF16)
+        for piece in pieces(jnp.where(spread, cosine[j : j + 1], F32(0.0))):
+            result += dot(piece, place)
+    sim_ref[...] = result[:, 0:K]
+
+    arrive(W - 1)
 
     pairs = near_ref.shape[0]
     group = 8
@@ -268,24 +340,8 @@
     near_ref[...] = jnp.where(live, (low + info_s[rows[0]]) / features, F32(0.0))
     marg_ref[...] = jnp.where(live, (second - low) / features, F32(0.0))
 
-    loop(W - 1, 4, lambda d: part_copy(d).wait_recv())
-    total = part_out[W - 1]
-    for d in range(W - 1):
-        total += part_in[d]
-    cosine = total[0:J] / jnp.sqrt(total[2 * J : 2 * J + 1] * total[J : 2 * J])
-    spread = lax.broadcasted_iota(I32, (R, LANES), 1) % R == lax.broadcasted_iota(I32, (R, LANES), 0)
-    out_cols = ceil_to(K, LANES)
-    deep = lax.broadcasted_iota(I32, (LANES, out_cols), 0) // R
-    across = lax.broadcasted_iota(I32, (LANES, out_cols), 1)
-    result = jnp.zeros((R, out_cols), F32)
-    for j in range(J):
-        place = jnp.where(across == deep + j * KK, F32(1.0), F32(0.0)).astype(BF16)
-        for piece in pieces(jnp.where(spread, cosine[j : j + 1], F32(0.0))):
-            result += dot(piece, place)
-    sim_ref[...] = result[:, 0:K]
-
-    loop(n - 1, 16, lambda i: desc_copy(i + 1).wait_send())
-    loop(W - 1, 4, lambda d: part_copy(d).wait_send())
+    whole(outd.at[pl.ds(0, n - 1)], dsend, drecv.at[0]).wait_send()
+    whole(part_out.at[pl.ds(0, W - 1)], psend, precv).wait_send()
 
 
 def finish(*refs):
@@ -342,11 +398,12 @@
             pltpu.VMEM((pairs * 8, width), F32),
             pltpu.VMEM((pairs * 8, width), F32),
             pltpu.VMEM((pairs * 8, width), F32),
-            pltpu.SemaphoreType.DMA((W * S,)),
-            pltpu.SemaphoreType.DMA((W * S,)),
+            pltpu.SemaphoreType.DMA,
             pltpu.SemaphoreType.DMA((W,)),
-            pltpu.SemaphoreType.DMA((W,)),
+            pltpu.SemaphoreType.DMA,
+            pltpu.SemaphoreType.DMA,
             pltpu.SemaphoreType.DMA((8,)),
+            pltpu.SemaphoreType.REGULAR((W,)),
         ],
         compiler_params=pltpu.CompilerParams(
             collective_id=0, has_side_effects=True, vmem_limit_bytes=LIMIT

time: 16.2 us -> 14.6 us (0.901)
  Pallas kernels: 15.4 us -> 13.7 us
    pallas_call x1, Pallas kernels: 14.7 us -> 13.1 us  [local(): pl.pallas_call(functools.partial(kernel, W, S, (B, I, K, R, KK, J, C, TR,...]
where the time goes in v1:
time: 14.6 us; the launch traced here: 14.4 us
  Pallas kernels  13.7 us (94%)
  between operations  0.64 us (4%)
    pallas_call x1, Pallas kernels, local(): pl.pallas_call(functools.partial(kernel, W, S, (B, I, K, R, KK, J, C, TR,...  13.1 us
    pallas_call x1, Pallas kernels, local(): pl.pallas_call(finish, out_shape=tuple((jax.ShapeDtypeStruct(shape, F32)...  0.64 us

profile of v1, /device:TPU:0, one launch (start us, length us, event | category | flops | bytes accessed | tf_op | source)
XLA Modules:
  0.0 14.4 jit_solution(1094353156287304433)
XLA Ops:
  0.6 13.1 %shard_map.94 = (f32[16,50]{1,0:T(8,128)S(1)}, f32[32,128]{1,0:T(8,128)S(1)}, f32[32,128]{1,0:T(8,128)S(1)}) custom-call(s32[32,256]{1,0:T(8,128)} %bitcast.8, f32[32,256]{1,0:T(8,128)} %bitcast.9, s32[50,256]{1,0:T(8,128)} %nb_hbm.1, bf16[64,32,128]{2,1,0:T(8,128)(2,1)} %desc_hbm.1, s32[256]{0:T(256)} %cnt_hbm.1, s32[4,4,2,4]{3,2,1,0:T(2,128)} %bitcast.10, ...), custom_call_target="tpu_custom_call" | custom-call | tf_op jit(solution)/shard_map/pallas_call | solution.py:371
  13.7 0.6 %shard_map.95 = (f32[16,50]{1,0:T(8,128)}, f32[32,128]{1,0:T(8,128)}, f32[32,128]{1,0:T(8,128)}) custom-call(f32[16,50]{1,0:T(8,128)S(1)} %get-tuple-element.9.refs_0_, f32[32,128]{1,0:T(8,128)S(1)} %get-tuple-element.10.refs_1_, f32[32,128]{1,0:T(8,128)S(1)} %get-tuple-element.11.refs_2_), custom_call_target="tpu_custom_call" | custom-call | tf_op jit(solution)/shard_map/pallas_call | solution.py:415

commit v2 on v1

--- a/solution.py
+++ b/solution.py
@@ -47,29 +47,35 @@
     ids_hbm, wts_hbm, nb_hbm, desc_hbm, cnt_hbm, tab_hbm, slot_hbm,
     sim_ref, near_ref, marg_ref,
     ids_ref, wts_ref, nb_ref, desc_ref, cnt_ref, to_ref, from_ref, slot_ref,
-    outd, held, table, nbf, own, hot, got, part_out, part_in,
+    outd, held, table, nbf, own, wanted, got_0, got_1, part_out, part_in,
     qs, rt, sqb, info, low_s, next_s, info_s,
     dsend, drecv, psend, precv, inputs, go,
 ):
     B, I, K, R, KK, J, C, TR, KP, NP, H = dims
+    gots = got_0, got_1
     me_g, me_w, me_s = lax.axis_index("groups"), lax.axis_index("word"), lax.axis_index("sub")
     n = W * S
     stored, feats, width = desc_ref.shape
 
     def turn(step):
-        if W & (W - 1):
-            return (me_w + step) % W
-        word, bit = me_w, 1
-        while bit < W:
-            word += step // bit % 2 * (1 - me_w // bit % 2 * 2) * bit
-            bit *= 2
-        return word
+        if isinstance(step, int) and step == 0:
+            return me_w
+        base = jnp.where(me_w == W // 2 - 1, 0, W // 2)
+        place = (me_w - base + W) % W
+        w = (base + step - 1 + jnp.where(step > place, 1, 0)) % W
+        return w if isinstance(step, int) else jnp.where(step == 0, me_w, w)
 
     def word_at(k):
         return k + jnp.where(me_w <= k, 1, 0)
 
-    def near(j):
-        return (me_s + 1 + j) % S
+    def sub_at(j):
+        if S & (S - 1):
+            return (me_s + j) % S
+        sub, bit = me_s, 1
+        while bit < S:
+            sub += (S - 1 - j) // bit % 2 * (1 - me_s // bit % 2 * 2) * bit
+            bit *= 2
+        return sub
 
     def load(sem, source, target):
         return pltpu.make_async_copy(source, target, inputs.at[sem])
@@ -116,8 +122,8 @@
         for c in range(C):
             outd[slot, c] = desc_ref[to_ref[w, c, s]]
 
-    loop(W - 1, 4, lambda k: loop(S, 8, lambda s: pick(k * S + s, word_at(k), s)))
-    loop(S, 8, lambda s: pick((W - 1) * S + s, me_w, s))
+    loop(W - 1, 4, lambda k: loop(S, 8, lambda j: pick(k * S + j, word_at(k), sub_at(j))))
+    loop(S, 8, lambda j: pick((W - 1) * S + j, me_w, sub_at(j)))
     for c in range(C):
         held[me_w, me_s, c] = desc_ref[to_ref[me_w, c, me_s]]
 
@@ -129,13 +135,17 @@
         ).start()
 
     def send_word(k):
-        loop(S, 8, lambda s: send(k * S + s, word_at(k), s))
-
-    def send_near(s):
-        send((W - 1) * S + s, me_w, s)
+        loop(S, 8, lambda j: send(k * S + j, word_at(k), sub_at(j)))
+
+    def send_near(above):
+        def each(j):
+            s = sub_at(j)
+            pl.when((s > me_s) if above else (s < me_s))(lambda: send((W - 1) * S + j, me_w, s))
+
+        loop(S, 8, each)
 
     pl.when(me_w > 0)(lambda: send_word(0))
-    subs(False, send_near)
+    send_near(False)
 
     for copy in rest:
         copy.wait()
@@ -177,33 +187,42 @@
         )
 
     early = 2 * me_w < W - 1
-
-    def due(d):
-        low = jnp.logical_and(d >= 0, d < me_w)
-        high = jnp.logical_and(d >= me_w, d < W - 1)
-        return jnp.logical_or(low, jnp.logical_and(high, jnp.logical_not(early)))
-
     lane = lax.broadcasted_iota(I32, (1, LANES), 1)
     digit = lax.broadcasted_iota(I32, (KK, LANES), 0) == lax.broadcasted_iota(I32, (KK, LANES), 1) // R
 
-    def target(d):
+    def order(i):
+        d = (i + jnp.where(early, me_w, 0)) % max(W - 1, 1)
+        if isinstance(i, int):
+            return d if i < W - 1 else W - 1
+        return jnp.where(i < W - 1, d, W - 1)
+
+    def owned(i):
+        d = order(i)
         w = jnp.where(d == W - 1, me_w, word_at(d))
         mine = dot(table[...], onehot((w * S + me_s) * R + lane % R, I))
-        own[0:B] = mine[0:B] * 256.0 + mine[B : 2 * B]
-        own[B : 2 * B] = mine[2 * B : 3 * B] + mine[3 * B : 4 * B] + mine[4 * B : 5 * B]
+        own[i, 0:B] = mine[0:B] * 256.0 + mine[B : 2 * B]
+        own[i, B : 2 * B] = mine[2 * B : 3 * B] + mine[3 * B : 4 * B] + mine[4 * B : 5 * B]
+        own[i, 2 * B : 2 * B + 1] = (
+            mine[5 * B : 5 * B + 1] + mine[5 * B + 1 : 5 * B + 2] + mine[5 * B + 2 : 5 * B + 3]
+        )
         listed = mine[TR : TR + KP] * 256.0 + mine[TR + KP : TR + 2 * KP]
         for j in range(J):
             chosen = jnp.where(digit, listed[j * KK : (j + 1) * KK], F32(0.0))
-            want = jnp.sum(chosen, axis=0, keepdims=True).astype(I32)
-            hot[:, j * LANES : (j + 1) * LANES] = onehot(want, I)
-        pl.when(due(d - 1))(lambda: part_copy(d - 1).start())
-        pl.when(jnp.logical_and(d >= 1, d < me_w))(lambda: send_word(d))
-        got[...] = dot(table[0:TR], hot[...])
+            wanted[i, j : j + 1] = jnp.sum(chosen, axis=0, keepdims=True).astype(I32)
+
+    def gather(i):
+        got = gots[i % 2] if isinstance(i, int) else gots[0]
+        for j in range(J):
+            got[:, j * LANES : (j + 1) * LANES] = dot(table[0:TR], onehot(wanted[i, j : j + 1], I))
+
+    def target(i):
+        d = order(i)
+        got = gots[i % 2] if isinstance(i, int) else gots[0]
         cols = [slice(j * LANES, (j + 1) * LANES) for j in range(J)]
         words_of = [got[0:B, c] * 256.0 + got[B : 2 * B, c] for c in cols]
         total = [jnp.zeros((B, LANES), F32) for c in cols]
         for a in range(B):
-            word, weight = own[a : a + 1], own[B + a : B + a + 1]
+            word, weight = own[i, a : a + 1], own[i, B + a : B + a + 1]
             for j in range(J):
                 total[j] += jnp.where(words_of[j] == word, weight, F32(0.0))
         for j, c in enumerate(cols):
@@ -211,37 +230,46 @@
             part_out[d, j : j + 1] = jnp.sum(total[j] * values, axis=0, keepdims=True)
             norms = got[5 * B : 5 * B + 1, c] + got[5 * B + 1 : 5 * B + 2, c] + got[5 * B + 2 : 5 * B + 3, c]
             part_out[d, J + j : J + j + 1] = norms
-        part_out[d, 2 * J : 2 * J + 1] = (
-            mine[5 * B : 5 * B + 1] + mine[5 * B + 1 : 5 * B + 2] + mine[5 * B + 2 : 5 * B + 3]
-        )
-    def targets(first, last):
-        lax.fori_loop(first, last, lambda d, carry: (target(d), carry)[1], 0)
-
-    def quota(e):
-        return jnp.minimum(jnp.maximum(W - 2 - me_w + e, 1), W)
-
-    def stage(e):
-        targets(0 if isinstance(e, int) and e == 0 else jnp.where(e == 0, 0, quota(e - 1)), quota(e))
-        if not isinstance(e, int):
-            pl.when(e == 0)(near_stage)
-            pl.when(e > 0)(lambda: far_stage(e))
-        elif e == 0:
-            near_stage()
-        else:
-            far_stage(e)
-
-    def near_stage():
-        pl.when(me_s < S - 1)(lambda: pl.semaphore_wait(go.at[me_w], S - 1 - me_s))
-        subs(True, send_near)
-
-    def far_stage(e):
-        w = me_w + e
-        pl.semaphore_wait(go.at[w], S)
-        pl.when(early)(lambda: part_copy(w - 1).start())
-        send_word(w - 1)
-
-    loop(W, 4, lambda e: pl.when(me_w + e < W)(lambda: stage(e)))
-    targets(quota(W - 1 - me_w), W)
+        part_out[d, 2 * J : 2 * J + 1] = own[i, 2 * B : 2 * B + 1]
+
+    def far_sends():
+        def each(k):
+            @pl.when(k >= me_w)
+            def _():
+                pl.semaphore_wait(go.at[k + 1], S)
+                send_word(k)
+
+        loop(W - 1, 4, each)
+
+    def after(i):
+        d = order(i)
+        if isinstance(i, int) and i == 0:
+            pl.when(me_s < S - 1)(lambda: pl.semaphore_wait(go.at[me_w], S - 1 - me_s))
+            send_near(True)
+            pl.when(jnp.logical_not(early))(far_sends)
+        next_high = jnp.logical_and(early, me_w + 1 + i < W)
+        pl.when(next_high)(lambda: pl.semaphore_wait(go.at[me_w + 1 + i], S))
+        part_copy(d).start()
+        pl.when(next_high)(lambda: send_word(d))
+        pl.when(jnp.logical_and(jnp.logical_not(early), i + 1 < me_w))(lambda: send_word(me_w - 1 - i))
+
+    loop(W, 4, owned)
+    if W <= 4:
+        gather(0)
+        for i in range(W):
+            target(i)
+            if i + 1 < W:
+                gather(i + 1)
+                after(i)
+    else:
+        def step(i):
+            gather(i)
+            target(i)
+
+        step(0)
+        after(0)
+        lax.fori_loop(1, W - 1, lambda i, carry: (step(i), after(i), carry)[2], 0)
+        step(W - 1)
 
     def arrive(i):
         w = turn(i)
@@ -386,8 +414,9 @@
             pltpu.VMEM((W, S, C, feats, width), BF16),
             pltpu.VMEM((TR + 2 * KP, I), BF16),
             pltpu.VMEM((KP, I), I32),
-            pltpu.VMEM((2 * B, LANES), F32),
-            pltpu.VMEM((I, J * LANES), BF16),
+            pltpu.VMEM((W, 2 * B + 8, LANES), F32),
+            pltpu.VMEM((W, ceil_to(J, 8), LANES), I32),
+            pltpu.VMEM((TR, J * LANES), F32),
             pltpu.VMEM((TR, J * LANES), F32),
             pltpu.VMEM((W, NP, LANES), F32),
             pltpu.VMEM((W, NP, LANES), F32),

time: 14.6 us -> 13.6 us (0.932)
  the two profiles are of different devices: /device:TPU:0 before, /device:TPU:24 now
where the time goes in v2:
time: 13.6 us; the launch traced here: 13.4 us
  Pallas kernels  12.7 us (93%)
  between operations  0.64 us (5%)
    pallas_call x1, Pallas kernels, local(): pl.pallas_call(functools.partial(kernel, W, S, (B, I, K, R, KK, J, C, TR,...  12.1 us
    pallas_call x1, Pallas kernels, local(): pl.pallas_call(finish, out_shape=tuple((jax.ShapeDtypeStruct(shape, F32)...  0.64 us

profile of v2, /device:TPU:24, one launch (start us, length us, event | category | flops | bytes accessed | tf_op | source)
XLA Modules:
  0.0 13.4 jit_solution(9865112718068651076)
XLA Ops:
  0.6 12.1 %shard_map.94 = (f32[16,50]{1,0:T(8,128)S(1)}, f32[32,128]{1,0:T(8,128)S(1)}, f32[32,128]{1,0:T(8,128)S(1)}) custom-call(s32[32,256]{1,0:T(8,128)} %bitcast.8, f32[32,256]{1,0:T(8,128)} %bitcast.9, s32[50,256]{1,0:T(8,128)} %nb_hbm.1, bf16[64,32,128]{2,1,0:T(8,128)(2,1)} %desc_hbm.1, s32[256]{0:T(256)} %cnt_hbm.1, s32[4,4,2,4]{3,2,1,0:T(2,128)} %bitcast.10, ...), custom_call_target="tpu_custom_call" | custom-call | tf_op jit(solution)/shard_map/pallas_call | solution.py:399
  12.7 0.6 %shard_map.95 = (f32[16,50]{1,0:T(8,128)}, f32[32,128]{1,0:T(8,128)}, f32[32,128]{1,0:T(8,128)}) custom-call(f32[16,50]{1,0:T(8,128)S(1)} %get-tuple-element.9.refs_0_, f32[32,128]{1,0:T(8,128)S(1)} %get-tuple-element.10.refs_1_, f32[32,128]{1,0:T(8,128)S(1)} %get-tuple-element.11.refs_2_), custom_call_target="tpu_custom_call" | custom-call | tf_op jit(solution)/shard_map/pallas_call | solution.py:444

commit v3 on v2

--- a/solution.py
+++ b/solution.py
@@ -27,10 +27,7 @@
 
 def pieces(x):
     first = x.astype(BF16)
-    rest = x - first.astype(F32)
-    second = rest.astype(BF16)
-    third = (rest - second.astype(F32)).astype(BF16)
-    return first, second, third
+    return first, (x - first.astype(F32)).astype(BF16)
 
 
 def dot(a, b):
@@ -48,11 +45,12 @@
     sim_ref, near_ref, marg_ref,
     ids_ref, wts_ref, nb_ref, desc_ref, cnt_ref, to_ref, from_ref, slot_ref,
     outd, held, table, nbf, own, wanted, got_0, got_1, part_out, part_in,
-    qs, rt, sqb, info, low_s, next_s, info_s,
+    qs, rt, sqb, info, low_t, next_t, low_s, next_s, info_s,
     dsend, drecv, psend, precv, inputs, go,
 ):
     B, I, K, R, KK, J, C, TR, KP, NP, H = dims
     gots = got_0, got_1
+    gram = qs.shape[0] == W
     me_g, me_w, me_s = lax.axis_index("groups"), lax.axis_index("word"), lax.axis_index("sub")
     n = W * S
     stored, feats, width = desc_ref.shape
@@ -60,9 +58,10 @@
     def turn(step):
         if isinstance(step, int) and step == 0:
             return me_w
-        base = jnp.where(me_w == W // 2 - 1, 0, W // 2)
-        place = (me_w - base + W) % W
-        w = (base + step - 1 + jnp.where(step > place, 1, 0)) % W
+        inner = early
+        place = jnp.where(inner, W - me_w, me_w + W - W // 2) % W
+        k = step - 1 + jnp.where(step > place, 1, 0)
+        w = jnp.where(inner, W - k, W // 2 + k) % W
         return w if isinstance(step, int) else jnp.where(step == 0, me_w, w)
 
     def word_at(k):
@@ -82,15 +81,15 @@
 
     first = [
         load(0, tab_hbm.at[me_w], to_ref),
-        load(1, desc_hbm, desc_ref),
+        load(0, desc_hbm, desc_ref),
     ]
     rest = [
-        load(2, ids_hbm, ids_ref),
-        load(3, wts_hbm, wts_ref),
-        load(4, nb_hbm, nb_ref),
-        load(5, tab_hbm.at[:, me_w], from_ref),
-        load(6, cnt_hbm, cnt_ref),
-        load(7, slot_hbm, slot_ref),
+        load(1, ids_hbm, ids_ref),
+        load(1, wts_hbm, wts_ref),
+        load(1, nb_hbm, nb_ref),
+        load(1, tab_hbm.at[:, me_w], from_ref),
+        load(1, cnt_hbm, cnt_ref),
+        load(1, slot_hbm, slot_ref),
     ]
     for copy in first:
         copy.start()
@@ -144,6 +143,8 @@
 
         loop(S, 8, each)
 
+    early = 2 * me_w < W - 1
+    late = jnp.logical_not(early)
     pl.when(me_w > 0)(lambda: send_word(0))
     send_near(False)
 
@@ -174,7 +175,7 @@
         block = jnp.zeros((16, chunk), F32)
         for k, piece in enumerate(pieces(norm)):
             block = jnp.where(row == k, piece.astype(F32), block)
-        table[5 * B : TR, at] = block.astype(BF16)
+        table[4 * B : TR, at] = block.astype(BF16)
 
     loop(I // chunk, 1, self_norm)
 
@@ -186,7 +187,6 @@
             device_id=(me_g, w, me_s), device_id_type=MESH,
         )
 
-    early = 2 * me_w < W - 1
     lane = lax.broadcasted_iota(I32, (1, LANES), 1)
     digit = lax.broadcasted_iota(I32, (KK, LANES), 0) == lax.broadcasted_iota(I32, (KK, LANES), 1) // R
 
@@ -201,10 +201,8 @@
         w = jnp.where(d == W - 1, me_w, word_at(d))
         mine = dot(table[...], onehot((w * S + me_s) * R + lane % R, I))
         own[i, 0:B] = mine[0:B] * 256.0 + mine[B : 2 * B]
-        own[i, B : 2 * B] = mine[2 * B : 3 * B] + mine[3 * B : 4 * B] + mine[4 * B : 5 * B]
-        own[i, 2 * B : 2 * B + 1] = (
-            mine[5 * B : 5 * B + 1] + mine[5 * B + 1 : 5 * B + 2] + mine[5 * B + 2 : 5 * B + 3]
-        )
+        own[i, B : 2 * B] = mine[2 * B : 3 * B] + mine[3 * B : 4 * B]
+        own[i, 2 * B : 2 * B + 1] = mine[4 * B : 4 * B + 1] + mine[4 * B + 1 : 4 * B + 2]
         listed = mine[TR : TR + KP] * 256.0 + mine[TR + KP : TR + 2 * KP]
         for j in range(J):
             chosen = jnp.where(digit, listed[j * KK : (j + 1) * KK], F32(0.0))
@@ -226,9 +224,9 @@
             for j in range(J):
                 total[j] += jnp.where(words_of[j] == word, weight, F32(0.0))
         for j, c in enumerate(cols):
-            values = got[2 * B : 3 * B, c] + got[3 * B : 4 * B, c] + got[4 * B : 5 * B, c]
+            values = got[2 * B : 3 * B, c] + got[3 * B : 4 * B, c]
             part_out[d, j : j + 1] = jnp.sum(total[j] * values, axis=0, keepdims=True)
-            norms = got[5 * B : 5 * B + 1, c] + got[5 * B + 1 : 5 * B + 2, c] + got[5 * B + 2 : 5 * B + 3, c]
+            norms = got[4 * B : 4 * B + 1, c] + got[4 * B + 1 : 4 * B + 2, c]
             part_out[d, J + j : J + j + 1] = norms
         part_out[d, 2 * J : 2 * J + 1] = own[i, 2 * B : 2 * B + 1]
 
@@ -246,12 +244,19 @@
         if isinstance(i, int) and i == 0:
             pl.when(me_s < S - 1)(lambda: pl.semaphore_wait(go.at[me_w], S - 1 - me_s))
             send_near(True)
-            pl.when(jnp.logical_not(early))(far_sends)
-        next_high = jnp.logical_and(early, me_w + 1 + i < W)
-        pl.when(next_high)(lambda: pl.semaphore_wait(go.at[me_w + 1 + i], S))
+            pl.when(late)(far_sends)
+        high = me_w + 1 + i < W
+        wait_high = jnp.logical_and(early, high)
+        pl.when(wait_high)(lambda: pl.semaphore_wait(go.at[me_w + 1 + i], S))
         part_copy(d).start()
-        pl.when(next_high)(lambda: send_word(d))
-        pl.when(jnp.logical_and(jnp.logical_not(early), i + 1 < me_w))(lambda: send_word(me_w - 1 - i))
+        pl.when(wait_high)(lambda: send_word(d))
+        rest_low = jnp.logical_and(jnp.logical_and(early, jnp.logical_not(high)), d > 0)
+        pl.when(rest_low)(lambda: send_word(d))
+        if isinstance(i, int) and i == 0:
+            pl.when(jnp.logical_and(late, me_w > 2))(lambda: send_word(me_w - 1))
+        else:
+            held_back = jnp.logical_or(i < me_w - 1, jnp.logical_and(i == 1, me_w == 2))
+            pl.when(jnp.logical_and(late, held_back))(lambda: send_word(i))
 
     loop(W, 4, owned)
     if W <= 4:
@@ -271,8 +276,39 @@
         lax.fori_loop(1, W - 1, lambda i, carry: (step(i), after(i), carry)[2], 0)
         step(W - 1)
 
+    pairs = near_ref.shape[0]
+    group = 8
+
+    order_of = [turn(i) for i in range(W)] if gram else None
+
+    def lowest_two(base, inner):
+        tops = []
+        for t in range(2):
+            low = second = None
+            for v in range(t, width // 8, 2):
+                x = base[v * 8 : v * 8 + 8] + inner[v * 8 : v * 8 + 8]
+                if low is None:
+                    low = x
+                elif second is None:
+                    low, second = jnp.minimum(low, x), jnp.maximum(low, x)
+                else:
+                    second = jnp.minimum(second, jnp.maximum(low, x))
+                    low = jnp.minimum(low, x)
+            tops.append((low, second))
+        (l0, s0), (l1, s1) = tops
+        return jnp.minimum(l0, l1), jnp.minimum(jnp.maximum(l0, l1), jnp.minimum(s0, s1))
+
+    def block(j, b):
+        inner = dot(rt[b], qs[j])
+        base = sqb[b]
+        for c in range(C):
+            a = j * C + c
+            if a != b:
+                cell = (order_of[j] * C + c) * H + order_of[b // C] * C + b % C
+                low_t[cell], next_t[cell] = lowest_two(base, inner[:, c * width : (c + 1) * width])
+
     def arrive(i):
-        w = turn(i)
+        w = order_of[i] if gram else turn(i)
 
         def arrived(slices):
             pltpu.make_async_remote_copy(
@@ -287,9 +323,12 @@
             pl.when(i > 0)(lambda: arrived(S))
             pl.when(i == 0)(lambda: arrived(S - 1))
         for c in range(C):
-            h = w * C + c
+            h = i * C + c if gram else w * C + c
             full = jnp.concatenate([held[w, s, c] for s in range(S)], axis=0)
-            qs[h] = full
+            if gram:
+                qs[i, :, c * width : (c + 1) * width] = full
+            else:
+                qs[h] = full
             wide = full.astype(F32)
             turned = jnp.transpose(wide)
             rt[h] = (turned * -2.0).astype(BF16)
@@ -299,9 +338,13 @@
             sqb[h] = jnp.where(down < count, square, F32(1e30))
             flat = jnp.sum(wide * wide, axis=0, keepdims=True)
             live = jnp.where(lax.broadcasted_iota(I32, (8, width), 1) < count, F32(1.0), F32(0.0))
-            info[h] = jnp.where(lax.broadcasted_iota(I32, (8, width), 0) == 0, flat, live)
-
-    loop(W - 1, 4, arrive)
+            info[w * C + c] = jnp.where(lax.broadcasted_iota(I32, (8, width), 0) == 0, flat, live)
+        if gram:
+            for b in range((i + 1) * C):
+                block(i, b)
+            for j in range(i):
+                for c in range(C):
+                    block(j, i * C + c)
 
     def whole(ref, send_sem, recv_sem):
         return pltpu.make_async_remote_copy(
@@ -309,51 +352,44 @@
             device_id=(me_g, me_w, me_s), device_id_type=MESH,
         )
 
-    whole(part_in.at[pl.ds(0, W - 1)], psend, precv).wait_recv()
-    total = part_out[W - 1]
-    for d in range(W - 1):
-        total += part_in[d]
-    cosine = total[0:J] / jnp.sqrt(total[2 * J : 2 * J + 1] * total[J : 2 * J])
-    spread = lax.broadcasted_iota(I32, (R, LANES), 1) % R == lax.broadcasted_iota(I32, (R, LANES), 0)
-    out_cols = ceil_to(K, LANES)
-    deep = lax.broadcasted_iota(I32, (LANES, out_cols), 0) // R
-    across = lax.broadcasted_iota(I32, (LANES, out_cols), 1)
-    result = jnp.zeros((R, out_cols), F32)
-    for j in range(J):
-        place = jnp.where(across == deep + j * KK, F32(1.0), F32(0.0)).astype(BF16)
-        for piece in pieces(jnp.where(spread, cosine[j : j + 1], F32(0.0))):
-            result += dot(piece, place)
-    sim_ref[...] = result[:, 0:K]
-
+    def similarity():
+        whole(part_in.at[pl.ds(0, W - 1)], psend, precv).wait_recv()
+        total = part_out[W - 1]
+        for d in range(W - 1):
+            total += part_in[d]
+        cosine = total[0:J] / jnp.sqrt(total[2 * J : 2 * J + 1] * total[J : 2 * J])
+        spread = lax.broadcasted_iota(I32, (R, LANES), 1) % R == lax.broadcasted_iota(I32, (R, LANES), 0)
+        out_cols = ceil_to(K, LANES)
+        deep = lax.broadcasted_iota(I32, (LANES, out_cols), 0) // R
+        across = lax.broadcasted_iota(I32, (LANES, out_cols), 1)
+        result = jnp.zeros((R, out_cols), F32)
+        for j in range(J):
+            place = jnp.where(across == deep + j * KK, F32(1.0), F32(0.0)).astype(BF16)
+            for piece in pieces(jnp.where(spread, cosine[j : j + 1], F32(0.0))):
+                result += dot(piece, place)
+        sim_ref[...] = result[:, 0:K]
+
+    if 2 < W <= 4:
+        arrive(0)
+        arrive(1)
+        pl.when(me_w == 0)(similarity)
+        loop(W - 3, 4, lambda i: arrive(2 + i))
+        pl.when(me_w > 0)(similarity)
+    else:
+        loop(W - 1, 4, arrive)
+        similarity()
     arrive(W - 1)
-
-    pairs = near_ref.shape[0]
-    group = 8
 
     def match(i):
         for k in range(group):
             p = i * group + k
-            q, r = slot_ref[0, p], slot_ref[1, p]
-            inner = dot(rt[r], qs[q])
-            base = sqb[r]
-            tops = []
-            for t in range(2):
-                low = second = None
-                for v in range(t, width // 8, 2):
-                    x = base[v * 8 : v * 8 + 8] + inner[v * 8 : v * 8 + 8]
-                    if low is None:
-                        low = x
-                    elif second is None:
-                        low, second = jnp.minimum(low, x), jnp.maximum(low, x)
-                    else:
-                        second = jnp.minimum(second, jnp.maximum(low, x))
-                        low = jnp.minimum(low, x)
-                tops.append((low, second))
-            (l0, s0), (l1, s1) = tops
+            a, b = slot_ref[0, p], slot_ref[1, p]
             at = pl.ds(p * 8, 8)
-            low_s[at] = jnp.minimum(l0, l1)
-            next_s[at] = jnp.minimum(jnp.maximum(l0, l1), jnp.minimum(s0, s1))
-            info_s[at] = info[q]
+            if gram:
+                low_s[at], next_s[at] = low_t[a * H + b], next_t[a * H + b]
+            else:
+                low_s[at], next_s[at] = lowest_two(sqb[b], dot(rt[b], qs[a]))
+            info_s[at] = info[a]
 
     loop(pairs // group, 4, match)
 
@@ -388,12 +424,13 @@
     KK = LANES // R
     J = -(-K // KK)
     C = send_table.shape[-1]
-    TR = ceil_to(5 * B + 3, 16)
+    TR = ceil_to(4 * B + 2, 16)
     KP = ceil_to(J * KK, 16)
     NP = ceil_to(2 * J + 1, 8)
     H = W * C
     stored, feats, width = descriptors.shape
     pairs = pair_slots.shape[2]
+    gram = W <= 4 and C > 1 and H * H <= 2 * pairs
     vmem = pl.BlockSpec(memory_space=pltpu.VMEM)
     results = ((R, K), (pairs, width), (pairs, width))
     parts = pl.pallas_call(
@@ -420,10 +457,12 @@
             pltpu.VMEM((TR, J * LANES), F32),
             pltpu.VMEM((W, NP, LANES), F32),
             pltpu.VMEM((W, NP, LANES), F32),
-            pltpu.VMEM((H, width, width), BF16),
+            pltpu.VMEM((W, width, C * width) if gram else (H, width, width), BF16),
             pltpu.VMEM((H, width, width), BF16),
             pltpu.VMEM((H, width, width), F32),
             pltpu.VMEM((H, 8, width), F32),
+            pltpu.VMEM((H * H if gram else 1, 8, width), F32),
+            pltpu.VMEM((H * H if gram else 1, 8, width), F32),
             pltpu.VMEM((pairs * 8, width), F32),
             pltpu.VMEM((pairs * 8, width), F32),
             pltpu.VMEM((pairs * 8, width), F32),
@@ -431,7 +470,7 @@
             pltpu.SemaphoreType.DMA((W,)),
             pltpu.SemaphoreType.DMA,
             pltpu.SemaphoreType.DMA,
-            pltpu.SemaphoreType.DMA((8,)),
+            pltpu.SemaphoreType.DMA((2,)),
             pltpu.SemaphoreType.REGULAR((W,)),
         ],
         compiler_params=pltpu.CompilerParams(

time: 13.6 us -> 13.3 us (0.978)
  Pallas kernels: 12.7 us -> 12.5 us
    pallas_call x1, Pallas kernels: 12.1 us -> 11.8 us  [local(): pl.pallas_call(functools.partial(kernel, W, S, (B, I, K, R, KK, J, C, TR,...]
where the time goes in v3:
time: 13.3 us; the launch traced here: 13.1 us
  Pallas kernels  12.5 us (94%)
  between operations  0.64 us (5%)
    pallas_call x1, Pallas kernels, local(): pl.pallas_call(functools.partial(kernel, W, S, (B, I, K, R, KK, J, C, TR,...  11.8 us
    pallas_call x1, Pallas kernels, local(): pl.pallas_call(finish, out_shape=tuple((jax.ShapeDtypeStruct(shape, F32)...  0.64 us

profile of v3, /device:TPU:24, one launch (start us, length us, event | category | flops | bytes accessed | tf_op | source)
XLA Modules:
  0.0 13.1 jit_solution(15595591975411891713)
XLA Ops:
  0.6 11.8 %shard_map.94 = (f32[16,50]{1,0:T(8,128)S(1)}, f32[32,128]{1,0:T(8,128)S(1)}, f32[32,128]{1,0:T(8,128)S(1)}) custom-call(s32[32,256]{1,0:T(8,128)} %bitcast.8, f32[32,256]{1,0:T(8,128)} %bitcast.9, s32[50,256]{1,0:T(8,128)} %nb_hbm.1, bf16[64,32,128]{2,1,0:T(8,128)(2,1)} %desc_hbm.1, s32[256]{0:T(256)} %cnt_hbm.1, s32[4,4,2,4]{3,2,1,0:T(2,128)} %bitcast.10, ...), custom_call_target="tpu_custom_call" | custom-call | tf_op jit(solution)/shard_map/pallas_call | solution.py:436
  12.5 0.6 %shard_map.95 = (f32[16,50]{1,0:T(8,128)}, f32[32,128]{1,0:T(8,128)}, f32[32,128]{1,0:T(8,128)}) custom-call(f32[16,50]{1,0:T(8,128)S(1)} %get-tuple-element.9.refs_0_, f32[32,128]{1,0:T(8,128)S(1)} %get-tuple-element.10.refs_1_, f32[32,128]{1,0:T(8,128)S(1)} %get-tuple-element.11.refs_2_), custom_call_target="tpu_custom_call" | custom-call | tf_op jit(solution)/shard_map/pallas_call | solution.py:483

commit v4 on v3

--- a/solution.py
+++ b/solution.py
@@ -106,13 +106,26 @@
     def signal(sem, w, s):
         pl.semaphore_signal(sem, inc=1, device_id=(me_g, w, s), device_id_type=MESH)
 
+    half, mid = S // 2, W // 2
+    paired = W > 1 and S > 1 and not W & (W - 1) and not S & (S - 1)
+    below, above = jnp.logical_and(paired, me_w == mid - 1), jnp.logical_and(paired, me_w == mid)
+    side = me_s // max(half, 1) * half
+
     subs(True, lambda s: signal(barrier, me_w, s))
+    if paired:
+        pl.when(above)(lambda: loop(half, 8, lambda j: signal(barrier, mid - 1, side + j)))
     words(True, lambda w: loop(S, 8, lambda s: signal(barrier, w, s)))
     for copy in rest:
         copy.start()
-    lower = me_w * S + me_s
+    lower = me_w * S + me_s + jnp.where(below, half, 0)
     pl.when(lower > 0)(lambda: pl.semaphore_wait(barrier, lower))
-    words(False, lambda w: loop(S, 8, lambda s: signal(go.at[me_w], w, s)))
+    def answer(w):
+        mate = jnp.logical_and(above, w == mid - 1)
+        if paired:
+            pl.when(mate)(lambda: loop(half, 8, lambda j: signal(go.at[me_w], w, half - side + j)))
+        pl.when(jnp.logical_not(mate))(lambda: loop(S, 8, lambda s: signal(go.at[me_w], w, s)))
+
+    words(False, answer)
     subs(False, lambda s: signal(go.at[me_w], me_w, s))
     for copy in first:
         copy.wait()
@@ -133,8 +146,8 @@
             device_id=(me_g, w, s), device_id_type=MESH,
         ).start()
 
-    def send_word(k):
-        loop(S, 8, lambda j: send(k * S + j, word_at(k), sub_at(j)))
+    def send_word(k, first=0, last=S):
+        loop(last - first, 8, lambda j: send(k * S + first + j, word_at(k), sub_at(first + j)))
 
     def send_near(above):
         def each(j):
@@ -145,7 +158,12 @@
 
     early = 2 * me_w < W - 1
     late = jnp.logical_not(early)
-    pl.when(me_w > 0)(lambda: send_word(0))
+    left = me_s < half
+    if paired:
+        pl.when(below)(lambda: send_word(mid - 1, half, S))
+    pl.when(jnp.logical_and(me_w > 0, left))(lambda: send_word(0, half, S))
+    pl.when(me_w > 0)(lambda: send_word(0, 0, half))
+    pl.when(jnp.logical_and(me_w > 0, jnp.logical_not(left)))(lambda: send_word(0, half, S))
     send_near(False)
 
     for copy in rest:
@@ -247,9 +265,13 @@
             pl.when(late)(far_sends)
         high = me_w + 1 + i < W
         wait_high = jnp.logical_and(early, high)
-        pl.when(wait_high)(lambda: pl.semaphore_wait(go.at[me_w + 1 + i], S))
+        mate = jnp.logical_and(below, i == 0)
+        pl.when(wait_high)(lambda: pl.semaphore_wait(go.at[me_w + 1 + i], jnp.where(mate, half, S)))
         part_copy(d).start()
-        pl.when(wait_high)(lambda: send_word(d))
+        full = jnp.logical_and(wait_high, jnp.logical_not(mate))
+        pl.when(jnp.logical_and(full, left))(lambda: send_word(d, half, S))
+        pl.when(wait_high)(lambda: send_word(d, 0, half))
+        pl.when(jnp.logical_and(full, jnp.logical_not(left)))(lambda: send_word(d, half, S))
         rest_low = jnp.logical_and(jnp.logical_and(early, jnp.logical_not(high)), d > 0)
         pl.when(rest_low)(lambda: send_word(d))
         if isinstance(i, int) and i == 0:
@@ -370,11 +392,8 @@
         sim_ref[...] = result[:, 0:K]
 
     if 2 < W <= 4:
-        arrive(0)
-        arrive(1)
-        pl.when(me_w == 0)(similarity)
-        loop(W - 3, 4, lambda i: arrive(2 + i))
-        pl.when(me_w > 0)(similarity)
+        loop(W - 1, 4, arrive)
+        pl.when(me_w >= 0)(similarity)
     else:
         loop(W - 1, 4, arrive)
         similarity()

time: 13.3 us -> 12.9 us (0.970)
  the two profiles are of different devices: /device:TPU:24 before, /device:TPU:0 now
where the time goes in v4:
time: 12.9 us; the launch traced here: 12.7 us
  Pallas kernels  12.1 us (94%)
  between operations  0.64 us (5%)
    pallas_call x1, Pallas kernels, local(): pl.pallas_call(functools.partial(kernel, W, S, (B, I, K, R, KK, J, C, TR,...  11.4 us
    pallas_call x1, Pallas kernels, local(): pl.pallas_call(finish, out_shape=tuple((jax.ShapeDtypeStruct(shape, F32)...  0.64 us

profile of v4, /device:TPU:0, one launch (start us, length us, event | category | flops | bytes accessed | tf_op | source)
XLA Modules:
  0.0 12.7 jit_solution(2802875377778532802)
XLA Ops:
  0.6 11.4 %shard_map.94 = (f32[16,50]{1,0:T(8,128)S(1)}, f32[32,128]{1,0:T(8,128)S(1)}, f32[32,128]{1,0:T(8,128)S(1)}) custom-call(s32[32,256]{1,0:T(8,128)} %bitcast.8, f32[32,256]{1,0:T(8,128)} %bitcast.9, s32[50,256]{1,0:T(8,128)} %nb_hbm.1, bf16[64,32,128]{2,1,0:T(8,128)(2,1)} %desc_hbm.1, s32[256]{0:T(256)} %cnt_hbm.1, s32[4,4,2,4]{3,2,1,0:T(2,128)} %bitcast.10, ...), custom_call_target="tpu_custom_call" | custom-call | tf_op jit(solution)/shard_map/pallas_call | solution.py:455
  12.1 0.6 %shard_map.95 = (f32[16,50]{1,0:T(8,128)}, f32[32,128]{1,0:T(8,128)}, f32[32,128]{1,0:T(8,128)}) custom-call(f32[16,50]{1,0:T(8,128)S(1)} %get-tuple-element.9.refs_0_, f32[32,128]{1,0:T(8,128)S(1)} %get-tuple-element.10.refs_1_, f32[32,128]{1,0:T(8,128)S(1)} %get-tuple-element.11.refs_2_), custom_call_target="tpu_custom_call" | custom-call | tf_op jit(solution)/shard_map/pallas_call | solution.py:502

commit v5 on v4

--- a/solution.py
+++ b/solution.py
@@ -46,7 +46,7 @@
     ids_ref, wts_ref, nb_ref, desc_ref, cnt_ref, to_ref, from_ref, slot_ref,
     outd, held, table, nbf, own, wanted, got_0, got_1, part_out, part_in,
     qs, rt, sqb, info, low_t, next_t, low_s, next_s, info_s,
-    dsend, drecv, psend, precv, inputs, go,
+    dsend, drecv, psend, precv, go,
 ):
     B, I, K, R, KK, J, C, TR, KP, NP, H = dims
     gots = got_0, got_1
@@ -77,19 +77,19 @@
         return sub
 
     def load(sem, source, target):
-        return pltpu.make_async_copy(source, target, inputs.at[sem])
+        return pltpu.make_async_copy(source, target, sem)
 
     first = [
-        load(0, tab_hbm.at[me_w], to_ref),
-        load(0, desc_hbm, desc_ref),
+        load(dsend, tab_hbm.at[me_w], to_ref),
+        load(dsend, desc_hbm, desc_ref),
     ]
     rest = [
-        load(1, ids_hbm, ids_ref),
-        load(1, wts_hbm, wts_ref),
-        load(1, nb_hbm, nb_ref),
-        load(1, tab_hbm.at[:, me_w], from_ref),
-        load(1, cnt_hbm, cnt_ref),
-        load(1, slot_hbm, slot_ref),
+        load(psend, ids_hbm, ids_ref),
+        load(psend, wts_hbm, wts_ref),
+        load(psend, nb_hbm, nb_ref),
+        load(psend, tab_hbm.at[:, me_w], from_ref),
+        load(psend, cnt_hbm, cnt_ref),
+        load(psend, slot_hbm, slot_ref),
     ]
     for copy in first:
         copy.start()
@@ -392,12 +392,16 @@
         sim_ref[...] = result[:, 0:K]
 
     if 2 < W <= 4:
-        loop(W - 1, 4, arrive)
-        pl.when(me_w >= 0)(similarity)
+        arrive(0)
+        arrive(1)
+        pl.when(me_w % 2 == 1)(similarity)
+        loop(W - 3, 4, lambda i: arrive(2 + i))
+        pl.when(me_w % 2 == 0)(similarity)
+        arrive(W - 1)
     else:
         loop(W - 1, 4, arrive)
         similarity()
-    arrive(W - 1)
+        arrive(W - 1)
 
     def match(i):
         for k in range(group):
@@ -489,7 +493,6 @@
             pltpu.SemaphoreType.DMA((W,)),
             pltpu.SemaphoreType.DMA,
             pltpu.SemaphoreType.DMA,
-            pltpu.SemaphoreType.DMA((2,)),
             pltpu.SemaphoreType.REGULAR((W,)),
         ],
         compiler_params=pltpu.CompilerParams(

time: 12.9 us -> 12.9 us (level)
  no operation moved by 1% of the time
where the time goes in v5:
time: 12.9 us; the launch traced here: 12.7 us
  Pallas kernels  12.1 us (94%)
  between operations  0.64 us (5%)
    pallas_call x1, Pallas kernels, local(): pl.pallas_call(functools.partial(kernel, W, S, (B, I, K, R, KK, J, C, TR,...  11.4 us
    pallas_call x1, Pallas kernels, local(): pl.pallas_call(finish, out_shape=tuple((jax.ShapeDtypeStruct(shape, F32)...  0.64 us

profile of v5, /device:TPU:0, one launch (start us, length us, event | category | flops | bytes accessed | tf_op | source)
XLA Modules:
  0.0 12.7 jit_solution(8759181067492008267)
XLA Ops:
  0.6 11.4 %shard_map.94 = (f32[16,50]{1,0:T(8,128)S(1)}, f32[32,128]{1,0:T(8,128)S(1)}, f32[32,128]{1,0:T(8,128)S(1)}) custom-call(s32[32,256]{1,0:T(8,128)} %bitcast.8, f32[32,256]{1,0:T(8,128)} %bitcast.9, s32[50,256]{1,0:T(8,128)} %nb_hbm.1, bf16[64,32,128]{2,1,0:T(8,128)(2,1)} %desc_hbm.1, s32[256]{0:T(256)} %cnt_hbm.1, s32[4,4,2,4]{3,2,1,0:T(2,128)} %bitcast.10, ...), custom_call_target="tpu_custom_call" | custom-call | tf_op jit(solution)/shard_map/pallas_call | solution.py:459
  12.1 0.6 %shard_map.95 = (f32[16,50]{1,0:T(8,128)}, f32[32,128]{1,0:T(8,128)}, f32[32,128]{1,0:T(8,128)}) custom-call(f32[16,50]{1,0:T(8,128)S(1)} %get-tuple-element.9.refs_0_, f32[32,128]{1,0:T(8,128)S(1)} %get-tuple-element.10.refs_1_, f32[32,128]{1,0:T(8,128)S(1)} %get-tuple-element.11.refs_2_), custom_call_target="tpu_custom_call" | custom-call | tf_op jit(solution)/shard_map/pallas_call | solution.py:505

commit v6 on v5

--- a/solution.py
+++ b/solution.py
@@ -68,13 +68,12 @@
         return k + jnp.where(me_w <= k, 1, 0)
 
     def sub_at(j):
-        if S & (S - 1):
+        if S % 2:
             return (me_s + j) % S
-        sub, bit = me_s, 1
-        while bit < S:
-            sub += (S - 1 - j) // bit % 2 * (1 - me_s // bit % 2 * 2) * bit
-            bit *= 2
-        return sub
+        own_side = me_s // (S // 2) * (S // 2)
+        if isinstance(j, int):
+            return S // 2 - own_side + j if j < S // 2 else own_side + j - S // 2
+        return jnp.where(j < S // 2, S // 2 - own_side + j, own_side + j - S // 2)
 
     def load(sem, source, target):
         return pltpu.make_async_copy(source, target, sem)
@@ -396,8 +395,9 @@
         arrive(1)
         pl.when(me_w % 2 == 1)(similarity)
         loop(W - 3, 4, lambda i: arrive(2 + i))
-        pl.when(me_w % 2 == 0)(similarity)
+        pl.when(jnp.logical_and(me_w % 2 == 0, me_w > 0))(similarity)
         arrive(W - 1)
+        pl.when(me_w == 0)(similarity)
     else:
         loop(W - 1, 4, arrive)
         similarity()
@@ -423,9 +423,9 @@
         second = jnp.minimum(jnp.maximum(low, l1), jnp.minimum(second, s1))
         low = jnp.minimum(low, l1)
     live = info_s[rows[1]] > 0.0
-    features = F32(feats * S)
-    near_ref[...] = jnp.where(live, (low + info_s[rows[0]]) / features, F32(0.0))
-    marg_ref[...] = jnp.where(live, (second - low) / features, F32(0.0))
+    scale = F32(1.0 / (feats * S))
+    near_ref[...] = jnp.where(live, (low + info_s[rows[0]]) * scale, F32(0.0))
+    marg_ref[...] = jnp.where(live, (second - low) * scale, F32(0.0))
 
     whole(outd.at[pl.ds(0, n - 1)], dsend, drecv.at[0]).wait_send()
     whole(part_out.at[pl.ds(0, W - 1)], psend, precv).wait_send()

time: 12.9 us -> 12.7 us (0.984)
  Pallas kernels: 12.1 us -> 11.9 us
    pallas_call x1, Pallas kernels: 11.4 us -> 11.3 us  [local(): pl.pallas_call(functools.partial(kernel, W, S, (B, I, K, R, KK, J, C, TR,...]
where the time goes in v6:
time: 12.7 us; the launch traced here: 12.5 us
  Pallas kernels  11.9 us (94%)
  between operations  0.64 us (5%)
    pallas_call x1, Pallas kernels, local(): pl.pallas_call(functools.partial(kernel, W, S, (B, I, K, R, KK, J, C, TR,...  11.3 us
    pallas_call x1, Pallas kernels, local(): pl.pallas_call(finish, out_shape=tuple((jax.ShapeDtypeStruct(shape, F32)...  0.64 us

profile of v6, /device:TPU:0, one launch (start us, length us, event | category | flops | bytes accessed | tf_op | source)
XLA Modules:
  0.0 12.5 jit_solution(9046560585303438974)
XLA Ops:
  0.6 11.3 %shard_map.94 = (f32[16,50]{1,0:T(8,128)S(1)}, f32[32,128]{1,0:T(8,128)S(1)}, f32[32,128]{1,0:T(8,128)S(1)}) custom-call(s32[32,256]{1,0:T(8,128)} %bitcast.8, f32[32,256]{1,0:T(8,128)} %bitcast.9, s32[50,256]{1,0:T(8,128)} %nb_hbm.1, bf16[64,32,128]{2,1,0:T(8,128)(2,1)} %desc_hbm.1, s32[256]{0:T(256)} %cnt_hbm.1, s32[4,4,2,4]{3,2,1,0:T(2,128)} %bitcast.10, ...), custom_call_target="tpu_custom_call" | custom-call | tf_op jit(solution)/shard_map/pallas_call | solution.py:459
  11.9 0.6 %shard_map.95 = (f32[16,50]{1,0:T(8,128)}, f32[32,128]{1,0:T(8,128)}, f32[32,128]{1,0:T(8,128)}) custom-call(f32[16,50]{1,0:T(8,128)S(1)} %get-tuple-element.9.refs_0_, f32[32,128]{1,0:T(8,128)S(1)} %get-tuple-element.10.refs_1_, f32[32,128]{1,0:T(8,128)S(1)} %get-tuple-element.11.refs_2_), custom_call_target="tpu_custom_call" | custom-call | tf_op jit(solution)/shard_map/pallas_call | solution.py:505

commit v7 on v6

--- a/solution.py
+++ b/solution.py
@@ -158,11 +158,11 @@
     early = 2 * me_w < W - 1
     late = jnp.logical_not(early)
     left = me_s < half
-    if paired:
-        pl.when(below)(lambda: send_word(mid - 1, half, S))
     pl.when(jnp.logical_and(me_w > 0, left))(lambda: send_word(0, half, S))
     pl.when(me_w > 0)(lambda: send_word(0, 0, half))
     pl.when(jnp.logical_and(me_w > 0, jnp.logical_not(left)))(lambda: send_word(0, half, S))
+    if paired:
+        pl.when(below)(lambda: send_word(mid - 1, half, S))
     send_near(False)
 
     for copy in rest:

time: 12.7 us -> 12.7 us (level)
  no operation moved by 1% of the time
where the time goes in v7:
time: 12.7 us; the launch traced here: 12.5 us
  Pallas kernels  11.9 us (94%)
  between operations  0.64 us (5%)
    pallas_call x1, Pallas kernels, local(): pl.pallas_call(functools.partial(kernel, W, S, (B, I, K, R, KK, J, C, TR,...  11.2 us
    pallas_call x1, Pallas kernels, local(): pl.pallas_call(finish, out_shape=tuple((jax.ShapeDtypeStruct(shape, F32)...  0.64 us

profile of v7, /device:TPU:0, one launch (start us, length us, event | category | flops | bytes accessed | tf_op | source)
XLA Modules:
  0.0 12.5 jit_solution(15753704451601979193)
XLA Ops:
  0.6 11.2 %shard_map.94 = (f32[16,50]{1,0:T(8,128)S(1)}, f32[32,128]{1,0:T(8,128)S(1)}, f32[32,128]{1,0:T(8,128)S(1)}) custom-call(s32[32,256]{1,0:T(8,128)} %bitcast.8, f32[32,256]{1,0:T(8,128)} %bitcast.9, s32[50,256]{1,0:T(8,128)} %nb_hbm.1, bf16[64,32,128]{2,1,0:T(8,128)(2,1)} %desc_hbm.1, s32[256]{0:T(256)} %cnt_hbm.1, s32[4,4,2,4]{3,2,1,0:T(2,128)} %bitcast.10, ...), custom_call_target="tpu_custom_call" | custom-call | tf_op jit(solution)/shard_map/pallas_call | solution.py:459
  11.9 0.6 %shard_map.95 = (f32[16,50]{1,0:T(8,128)}, f32[32,128]{1,0:T(8,128)}, f32[32,128]{1,0:T(8,128)}) custom-call(f32[16,50]{1,0:T(8,128)S(1)} %get-tuple-element.9.refs_0_, f32[32,128]{1,0:T(8,128)S(1)} %get-tuple-element.10.refs_1_, f32[32,128]{1,0:T(8,128)S(1)} %get-tuple-element.11.refs_2_), custom_call_target="tpu_custom_call" | custom-call | tf_op jit(solution)/shard_map/pallas_call | solution.py:505
